TPU v7x, 1024 devices: a whole 8x8x8 slice. The times are simulated.
1024 devices in a mesh: gx: 8 (over z), gy: 8 (over x), gz: 16 (over y, core).
Axes of the slice: x: 8, y: 8, z: 8, core: 2. Of those that a mesh axis runs over, the one named last changes fastest.
Arguments:
- fine_rhs: float32 [3072, 32, 1024], P(('gx', 'gy', 'gz')), may hold values from -6 to 6
- coarse_rhs: float32 [256, 256, 2048], P('gx', 'gy', 'gz'), may hold values from -6 to 6
- patch_count: int32 [1024], P(('gx', 'gy', 'gz')), may hold values from 2 to 3, as said below
- patch_corner: int32 [3072, 3], P(('gx', 'gy', 'gz')), may hold values from 0 to 2032, as said below
Outputs:
- fine_solution: float32 [3072, 32, 1024], P(('gx', 'gy', 'gz'))
- coarse_solution: float32 [256, 256, 2048], P('gx', 'gy', 'gz')
Inputs may be any that keep to these rules, and one draw needn't show every extreme that they name: Slots 0 to patch_count[d] - 1 of device d hold live patches, the others are unused. `patch_corner`: A live patch's footprint starts at a multiple of 16 in each dimension and lies inside the coarse block of one device with the same gx and gy indices as the patch's owner; live footprints never intersect; at most 2 live patches of one device lie in the block of any one device. Rows of unused slots are zero.
All inputs are finite; a program needn't handle non-finite values.
Results may differ from a plain program's by a relative error of at most 0.00007.
Values sent between devices are 32-bit elements; how exact they have to be, the bound alone decides.
A program may use at most 64 MiB of HBM per device.

v0:
```python
import jax
import jax.numpy as jnp
from jax import lax
from jax.sharding import PartitionSpec as P

CAP = 2
SWEEPS = 3
FINE_SWEEPS = 2


RELAX_WEIGHT = 0.9


def padded_2(cells, sides, width):
    for axis, dim in sides:
        count = lax.axis_size(axis)
        ends = count - 1
        head = lax.slice_in_dim(cells, 0, width, axis=dim)
        tail = lax.slice_in_dim(cells, cells.shape[dim] - width, cells.shape[dim], axis=dim)
        cells = jnp.concatenate(
            [
                lax.ppermute(tail, axis, [(i, (i + 1) % count) for i in range(ends)]),
                cells,
                lax.ppermute(head, axis, [((i + 1) % count, i) for i in range(ends)]),
            ],
            axis=dim,
        )
    return cells


def fine_neighbors(values_now, patch_edge):
    zero_first = jnp.zeros_like(values_now[:, :1])
    total = jnp.concatenate([values_now[:, 1:], zero_first], 1) + jnp.concatenate(
        [zero_first, values_now[:, :-1]], 1
    )
    zero_second = jnp.zeros_like(values_now[:, :, :patch_edge])
    total = total + jnp.concatenate([values_now[:, :, patch_edge:], zero_second], 2)
    total = total + jnp.concatenate([zero_second, values_now[:, :, :-patch_edge]], 2)
    zero_third = jnp.zeros_like(values_now[:, :, :1])
    depth_index = lax.broadcasted_iota(jnp.int32, (1, 1, values_now.shape[2]), 2) % patch_edge
    higher = jnp.concatenate([values_now[:, :, 1:], zero_third], 2)
    lower = jnp.concatenate([zero_third, values_now[:, :, :-1]], 2)
    total = total + jnp.where(depth_index < patch_edge - 1, higher, 0.0)
    return total + jnp.where(depth_index > 0, lower, 0.0)


def fine_relax(values_now, right_side, ghost_term, patch_edge):
    total = fine_neighbors(values_now, patch_edge)
    return values_now + RELAX_WEIGHT * (right_side + ghost_term - (6.0 * values_now - total)) / 6.0


def stencil(padded):
    total = padded[2:, 1:-1, 1:-1] + padded[:-2, 1:-1, 1:-1]
    total = total + padded[1:-1, 2:, 1:-1] + padded[1:-1, :-2, 1:-1]
    return total + padded[1:-1, 1:-1, 2:] + padded[1:-1, 1:-1, :-2]


def split_positions(block_values, foot_edge):
    cells_first, cells_second, cells_third = block_values.shape
    shaped = block_values.reshape(
        cells_first // foot_edge,
        foot_edge,
        cells_second // foot_edge,
        foot_edge,
        cells_third // foot_edge,
        foot_edge,
    )
    return shaped.transpose(0, 2, 4, 1, 3, 5).reshape(-1, foot_edge**3)


def merge_positions(position_rows, cells_first, cells_second, cells_third, foot_edge):
    shaped = position_rows.reshape(
        cells_first // foot_edge,
        cells_second // foot_edge,
        cells_third // foot_edge,
        foot_edge,
        foot_edge,
        foot_edge,
    )
    return shaped.transpose(0, 3, 1, 4, 2, 5).reshape(cells_first, cells_second, cells_third)


def domain_axis(device_index, group_count, cells, rim_width):
    offset = device_index * cells - rim_width
    indices = offset + jnp.arange(cells + 2 * rim_width, dtype=jnp.int32)
    return (indices >= 0) & (indices < cells * group_count)


def double_face(face_rows, foot_edge):
    shaped = face_rows.reshape(face_rows.shape[0], foot_edge, foot_edge)
    return jnp.repeat(jnp.repeat(shaped, 2, 1), 2, 2)


def per_device(fine_rhs, coarse_rhs, patch_count, patch_corner):
    slot_count, patch_edge, merged_edge = fine_rhs.shape
    foot_edge = patch_edge // 2
    cells_first, cells_second, cells_third = coarse_rhs.shape
    spots_first = cells_first // foot_edge
    spots_second = cells_second // foot_edge
    spots_third = cells_third // foot_edge
    spot_total = spots_first * spots_second * spots_third
    group_size = lax.axis_size("gz")
    slot_index = jnp.arange(slot_count, dtype=jnp.int32)
    alive_mask = slot_index < patch_count[0]
    merged_range = jnp.arange(merged_edge, dtype=jnp.int32)
    fine_second = merged_range // patch_edge
    fine_third = merged_range % patch_edge
    coarse_range = jnp.arange(foot_edge * foot_edge, dtype=jnp.int32)
    expand = ((fine_second // 2)[None, :] == (coarse_range // foot_edge)[:, None]) & (
        (fine_third // 2)[None, :] == (coarse_range % foot_edge)[:, None]
    )
    expand = expand.astype(jnp.float32)
    fine_iterate = jnp.zeros_like(fine_rhs)
    for iteration in range(FINE_SWEEPS):
        fine_iterate = fine_relax(fine_iterate, fine_rhs, 0.0, patch_edge)
    residual = fine_rhs - (6.0 * fine_iterate - fine_neighbors(fine_iterate, patch_edge))
    pairs = residual.reshape(slot_count, foot_edge, 2, merged_edge).sum(2)
    averages = 0.5 * lax.dot_general(
        pairs.reshape(slot_count * foot_edge, merged_edge),
        expand,
        (((1,), (1,)), ((), ())),
        precision=lax.Precision.HIGHEST,
    )
    averages = averages.reshape(slot_count, foot_edge**3)
    corner_first = patch_corner[:, 0]
    corner_second = patch_corner[:, 1]
    corner_third = patch_corner[:, 2]
    home_index = corner_third // cells_third
    spot_index = (
        corner_first % cells_first // foot_edge * spots_second
        + corner_second % cells_second // foot_edge
    ) * spots_third
    spot_index = spot_index + corner_third % cells_third // foot_edge
    spot_range = jnp.arange(spot_total, dtype=jnp.int32)
    earlier = (
        alive_mask[:, None] & alive_mask[None, :] & (home_index[:, None] == home_index[None, :])
    )
    earlier = earlier & (slot_index[None, :] < slot_index[:, None])
    rank_index = jnp.sum(earlier.astype(jnp.int32), 1)
    home_range = jnp.arange(group_size, dtype=jnp.int32)
    room_range = jnp.arange(CAP, dtype=jnp.int32)
    buckets = alive_mask[:, None, None] & (home_index[:, None, None] == home_range[None, :, None])
    buckets = buckets & (rank_index[:, None, None] == room_range[None, None, :])
    selector = buckets.astype(jnp.float32)
    outgoing = jnp.einsum("sgc,sv->gcv", selector, averages, precision=lax.Precision.HIGHEST)
    pair_rows = jnp.stack([spot_index, jnp.ones_like(spot_index)], 1)
    labels = jnp.sum(buckets.astype(jnp.int32)[:, :, :, None] * pair_rows[:, None, None, :], 0)
    arrived, arrived_tags = (
        lax.all_to_all(outgoing, "gz", split_axis=0, concat_axis=0, tiled=True),
        lax.all_to_all(labels, "gz", split_axis=0, concat_axis=0, tiled=True),
    )
    arrived = arrived.reshape(group_size * CAP, foot_edge**3)
    arrived_tags = arrived_tags.reshape(group_size * CAP, 2)
    placement = (
        (arrived_tags[:, 1:2] == 1) & (arrived_tags[:, 0:1] == spot_range[None, :])
    ).astype(jnp.float32)
    covered = jnp.sum(placement, 0)
    placed = jnp.dot(placement.T, arrived, precision=lax.Precision.HIGHEST)
    position_rows = jnp.where(
        covered[:, None] > 0.5, placed, split_positions(coarse_rhs, foot_edge)
    )
    composite = merge_positions(position_rows, cells_first, cells_second, cells_third, foot_edge)
    rim_width = SWEEPS
    widened = padded_2(composite, (("gx", 0), ("gy", 1), ("gz", 2)), rim_width)
    inside_first = domain_axis(lax.axis_index("gx"), lax.axis_size("gx"), cells_first, rim_width)
    inside_second = domain_axis(lax.axis_index("gy"), lax.axis_size("gy"), cells_second, rim_width)
    inside_third = domain_axis(lax.axis_index("gz"), lax.axis_size("gz"), cells_third, rim_width)
    inside = inside_first[:, None, None] & inside_second[None, :, None]
    inside = (inside & inside_third[None, None, :]).astype(jnp.float32)
    iterate = RELAX_WEIGHT * widened / 6.0
    for iteration in range(SWEEPS - 1):
        iterate = (
            iterate
            + RELAX_WEIGHT * (widened - (6.0 * iterate - stencil(jnp.pad(iterate, 1)))) / 6.0
        )
        iterate = iterate * inside
    solution = iterate[
        rim_width : rim_width + cells_first,
        rim_width : rim_width + cells_second,
        rim_width : rim_width + cells_third,
    ]
    padded = iterate[
        rim_width - 1 : rim_width + cells_first + 1,
        rim_width - 1 : rim_width + cells_second + 1,
        rim_width - 1 : rim_width + cells_third + 1,
    ]
    face_size = foot_edge * foot_edge
    interior = split_positions(padded[1:-1, 1:-1, 1:-1], foot_edge)

    def across_first(face_plane):
        shaped = face_plane.reshape(spots_first, spots_second, foot_edge, spots_third, foot_edge)
        return shaped.transpose(0, 1, 3, 2, 4).reshape(spot_total, face_size)

    def across_second(face_plane):
        shaped = face_plane.reshape(spots_first, foot_edge, spots_second, spots_third, foot_edge)
        return shaped.transpose(0, 2, 3, 1, 4).reshape(spot_total, face_size)

    def across_third(face_plane):
        shaped = face_plane.reshape(spots_first, foot_edge, spots_second, foot_edge, spots_third)
        return shaped.transpose(0, 2, 4, 1, 3).reshape(spot_total, face_size)

    low_first = across_first(
        padded[0:cells_first:foot_edge, 1 : cells_second + 1, 1 : cells_third + 1]
    )
    high_first = across_first(
        padded[
            foot_edge + 1 : cells_first + 2 : foot_edge, 1 : cells_second + 1, 1 : cells_third + 1
        ]
    )
    low_second = across_second(
        padded[1 : cells_first + 1, 0:cells_second:foot_edge, 1 : cells_third + 1]
    )
    high_second = across_second(
        padded[
            1 : cells_first + 1, foot_edge + 1 : cells_second + 2 : foot_edge, 1 : cells_third + 1
        ]
    )
    low_third = across_third(
        padded[1 : cells_first + 1, 1 : cells_second + 1, 0:cells_third:foot_edge]
    )
    high_third = across_third(
        padded[
            1 : cells_first + 1, 1 : cells_second + 1, foot_edge + 1 : cells_third + 2 : foot_edge
        ]
    )
    loop_table = jnp.concatenate(
        [interior, low_first, high_first, low_second, high_second, low_third, high_third], 1
    )
    outgoing_loop = jnp.dot(placement, loop_table, precision=lax.Precision.HIGHEST)
    returned = lax.all_to_all(
        outgoing_loop.reshape(group_size, CAP, -1), "gz", split_axis=0, concat_axis=0, tiled=True
    )
    loop_rows = jnp.einsum("sgc,gcv->sv", selector, returned, precision=lax.Precision.HIGHEST)
    cube_size = foot_edge**3
    parent_rows = loop_rows[:, :cube_size].reshape(slot_count * foot_edge, face_size)
    widened_parent = jnp.dot(parent_rows, expand, precision=lax.Precision.HIGHEST).reshape(
        slot_count, foot_edge, merged_edge
    )
    lifted = jnp.repeat(widened_parent, 2, 1)

    def face_part(number):
        return loop_rows[:, cube_size + number * face_size : cube_size + (number + 1) * face_size]

    first_index = lax.broadcasted_iota(jnp.int32, (1, patch_edge, 1), 1)
    low_x = jnp.dot(face_part(0), expand, precision=lax.Precision.HIGHEST)
    high_x = jnp.dot(face_part(1), expand, precision=lax.Precision.HIGHEST)
    ghost_term = jnp.where(first_index == 0, low_x[:, None, :], 0.0) + jnp.where(
        first_index == patch_edge - 1, high_x[:, None, :], 0.0
    )
    low_y = jnp.tile(double_face(face_part(2), foot_edge), (1, 1, patch_edge))
    high_y = jnp.tile(double_face(face_part(3), foot_edge), (1, 1, patch_edge))
    second_row = fine_second[None, None, :]
    ghost_term = (
        ghost_term
        + jnp.where(second_row == 0, low_y, 0.0)
        + jnp.where(second_row == patch_edge - 1, high_y, 0.0)
    )
    low_z = jnp.repeat(double_face(face_part(4), foot_edge), patch_edge, axis=2)
    high_z = jnp.repeat(double_face(face_part(5), foot_edge), patch_edge, axis=2)
    third_row = fine_third[None, None, :]
    ghost_term = (
        ghost_term
        + jnp.where(third_row == 0, low_z, 0.0)
        + jnp.where(third_row == patch_edge - 1, high_z, 0.0)
    )
    fine_iterate = fine_iterate + lifted
    for iteration in range(FINE_SWEEPS):
        fine_iterate = fine_relax(fine_iterate, fine_rhs, ghost_term, patch_edge)
    fine_solution = fine_iterate * alive_mask.astype(jnp.float32)[:, None, None]
    return (fine_solution, solution)


def solution(mesh):
    return jax.shard_map(
        per_device,
        mesh=mesh,
        in_specs=(
            P(("gx", "gy", "gz"), None, None),
            P("gx", "gy", "gz"),
            P(("gx", "gy", "gz")),
            P(("gx", "gy", "gz"), None),
        ),
        out_specs=(P(("gx", "gy", "gz"), None, None), P("gx", "gy", "gz")),
        check_vma=False,
    )
```

profile of v0, /device:TPU:1, one launch (start us, length us, event | category | flops | bytes accessed | tf_op | source)
XLA Modules:
  0.0 164.7 jit_solution(16627637761959210380)
XLA Ops:
  4.2 17.4 %all-to-all-start = ((s32[16,2,2]{1,2,0:T(2,128)}), s32[16,2,2]{1,2,0:T(2,128)S(1)}, u32[]{:S(2)}, u32[]{:S(2)}) async-start(s32[16,2,2]{1,2,0:T(2,128)} %copy.106), calls=%async_computation | async-start | bytes 32768 | tf_op jit(solution)/shard_map/all_to_all | solution.py:150
  29.0 6.9 %all-to-all-start.1 = ((f32[16,2,4096]{2,1,0:T(2,128)}), f32[16,2,4096]{2,1,0:T(2,128)S(1)}, u32[]{:S(2)}, u32[]{:S(2)}) async-start(f32[16,2,4096]{2,1,0:T(2,128)} %copy.108), calls=%async_computation.1 | async-start | bytes 1048576 | tf_op jit(solution)/shard_map/all_to_all | solution.py:149
  35.9 2.6 %reshape.461 = f32[2,16,2,16,8,16]{5,4,3,2,1,0:T(8,128)} reshape(f32[32,32,128]{2,1,0:T(8,128)S(1)} %copy-done.3) | data formatting | bytes 1048576 | tf_op jit(solution)/shard_map/reshape | solution.py:60
  38.5 5.0 %copy.143 = f32[2,16,2,16,8,16]{5,3,1,4,2,0:T(8,128)} copy(f32[2,16,2,16,8,16]{5,4,3,2,1,0:T(8,128)} %reshape.461) | data formatting | bytes 1048576 | tf_op jit(solution)/shard_map/reshape | solution.py:60
  43.5 4.7 %reshape.462 = f32[32,4096]{1,0:T(8,128)S(1)} reshape(f32[2,2,8,16,16,16]{5,4,3,2,1,0:T(8,128)} %bitcast.76) | data formatting | bytes 1048576 | tf_op jit(solution)/shard_map/reshape | solution.py:68
  48.4 4.7 %all-to-all-done.1 = f32[16,2,4096]{2,1,0:T(2,128)S(1)} async-done(((f32[16,2,4096]{2,1,0:T(2,128)}), f32[16,2,4096]{2,1,0:T(2,128)S(1)}, u32[]{:S(2)}, u32[]{:S(2)}) %all-to-all-start.1) | async-done | bytes 524320 | tf_op jit(solution)/shard_map/all_to_all | solution.py:149
  54.0 2.8 %reshape.463 = f32[2,2,8,16,16,16]{5,4,3,2,1,0:T(8,128)} reshape(f32[32,4096]{1,0:T(8,128)S(1)} %convolution_select_fusion) | data formatting | bytes 1048576 | tf_op jit(solution)/shard_map/reshape | solution.py:72
  56.8 6.6 %copy.142 = f32[2,2,8,16,16,16]{5,2,4,1,3,0:T(8,128)} copy(f32[2,2,8,16,16,16]{5,4,3,2,1,0:T(8,128)} %reshape.463) | data formatting | bytes 1048576 | tf_op jit(solution)/shard_map/reshape | solution.py:72
  63.4 3.2 %reshape.464 = f32[32,32,128]{2,1,0:T(8,128)S(1)} reshape(f32[2,16,2,16,8,16]{5,4,3,2,1,0:T(8,128)} %bitcast.77) | data formatting | bytes 1048576 | tf_op jit(solution)/shard_map/reshape | solution.py:80
  66.7 1.3 collective-permute-start
  68.0 1.3 collective-permute-start.1
  69.4 3.5 %collective-permute-done.1 = f32[3,32,128]{2,1,0:T(8,128)S(1)} collective-permute-done((f32[3,32,128]{2,1,0:T(8,128)S(1)}, f32[3,32,128]{2,1,0:T(8,128)S(1)}, u32[]{:S(2)}, u32[]{:S(2)}) %collective-permute-start.1) | collective-permute-done | bytes 49184 | tf_op jit(solution)/shard_map/ppermute | solution.py:24
  72.9 1.3 collective-permute-start.2
  74.2 1.3 collective-permute-start.3
  76.2 3.8 %collective-permute-done.3 = f32[38,3,128]{2,1,0:T(4,128)S(1)} collective-permute-done((f32[38,3,128]{2,1,0:T(4,128)S(1)}, f32[38,3,128]{2,1,0:T(4,128)S(1)}, u32[]{:S(2)}, u32[]{:S(2)}) %collective-permute-start.3) | collective-permute-done | bytes 58400 | tf_op jit(solution)/shard_map/ppermute | solution.py:24
  81.1 2.8 %collective-permute-start.5 = (f32[38,38,3]{1,0,2:T(8,128)S(1)}, f32[38,38,3]{1,0,2:T(8,128)S(1)}, u32[]{:S(2)}, u32[]{:S(2)}) collective-permute-start(f32[38,38,3]{1,0,2:T(8,128)S(1)} %copy.112), channel_id=1, source_target_pairs={{1,0},{2,1},{3,2},{4,3},{5,4},{6,5},{7,6},{8,7},{9,8},{10,9},{11,1... | collective-permute-start | bytes 51992 | tf_op jit(solution)/shard_map/ppermute | solution.py:24
  83.9 3.0 %collective-permute-start.4 = (f32[38,38,3]{1,0,2:T(8,128)S(1)}, f32[38,38,3]{1,0,2:T(8,128)S(1)}, u32[]{:S(2)}, u32[]{:S(2)}) collective-permute-start(f32[38,38,3]{1,0,2:T(8,128)S(1)} %copy.111), channel_id=1, source_target_pairs={{0,1},{1,2},{2,3},{3,4},{4,5},{5,6},{6,7},{7,8},{8,9},{9,10},{10,1... | collective-permute-start | bytes 51992 | tf_op jit(solution)/shard_map/ppermute | solution.py:22
  89.6 2.4 %and_select_fusion.1 = f32[38,38,134]{2,1,0:T(8,128)S(1)} fusion(f32[38,38,134]{2,1,0:T(8,128)S(1)} %broadcast_multiply_fusion, pred[134]{0:T(512)(128)(4,1)S(1)} %compare_and_fusion.1, pred[38,38]{1,0:T(8,128)(4,1)S(1)} %broadcast_and_fusion, f32[38,38,3]{2,1,0:T(8,128)S(1)} %copy.114, f32[38,3,128]{2,1,0:T(4,128)S(1)} %collective-permute-done.3, ...), kind=kLoop, calls=%fused_computation.5 | loop fusion | flops 3095936 | bytes 2323530 | tf_op jit(solution)/shard_map/mul | solution.py:176
  92.1 2.5 %and_select_fusion = f32[38,38,134]{2,1,0:T(8,128)S(1)} fusion(f32[38,38,134]{2,1,0:T(8,128)S(1)} %and_select_fusion.1, pred[134]{0:T(512)(128)(4,1)S(1)} %compare_and_fusion.1, pred[38,38]{1,0:T(8,128)(4,1)S(1)} %broadcast_and_fusion, f32[38,38,3]{2,1,0:T(8,128)S(1)} %copy.114, f32[38,3,128]{2,1,0:T(4,128)S(1)} %collective-permute-done.3, ...), kind=kLoop, calls=%fused_computation.4 | loop fusion | flops 3095936 | bytes 2323530 | tf_op jit(solution)/shard_map/mul | solution.py:176
  96.6 1.9 %slice.229 = f32[32,32,8]{2,1,0:T(8,128)S(1)} slice(f32[34,34,130]{2,1,0:T(8,128)S(1)} %slice.269), slice={[1:33:1], [1:33:1], [0:128:16]} | slice | bytes 65536 | tf_op jit(solution)/shard_map/slice | solution.py:219
  98.5 3.0 %slice.230 = f32[32,32,8]{2,1,0:T(8,128)} slice(f32[34,34,130]{2,1,0:T(8,128)S(1)} %slice.269), slice={[1:33:1], [1:33:1], [17:130:16]} | slice | bytes 65536 | tf_op jit(solution)/shard_map/slice | solution.py:222
  104.8 2.6 %reshape.465 = f32[2,16,2,16,8,16]{5,4,3,2,1,0:T(8,128)} reshape(f32[32,32,128]{2,1,0:T(8,128)S(1)} %slice.268) | data formatting | bytes 1048576 | tf_op jit(solution)/shard_map/reshape | solution.py:60
  107.4 5.0 %copy.115 = f32[2,2,8,16,16,16]{5,4,3,2,1,0:T(8,128)} copy(f32[2,2,8,16,16,16]{5,2,4,1,3,0:T(8,128)} %bitcast.78) | data formatting | bytes 1048576 | tf_op jit(solution)/shard_map/transpose | solution.py:68
  112.3 4.7 %reshape.466 = f32[32,4096]{1,0:T(8,128)S(1)} reshape(f32[2,2,8,16,16,16]{5,4,3,2,1,0:T(8,128)} %copy.115) | data formatting | bytes 1048576 | tf_op jit(solution)/shard_map/reshape | solution.py:68
  117.8 1.3 reshape.479
  119.1 6.4 %all-to-all-start.2 = ((f32[16,2,5632]{2,1,0:T(2,128)}), f32[16,2,5632]{2,1,0:T(2,128)S(1)}, u32[]{:S(2)}, u32[]{:S(2)}) async-start(f32[16,2,5632]{2,1,0:T(2,128)} %reshape.479), calls=%async_computation.2 | async-start | bytes 1441792 | tf_op jit(solution)/shard_map/all_to_all | solution.py:230
  125.6 21.3 %all-to-all-done.2 = f32[16,2,5632]{2,1,0:T(2,128)S(1)} async-done(((f32[16,2,5632]{2,1,0:T(2,128)}), f32[16,2,5632]{2,1,0:T(2,128)S(1)}, u32[]{:S(2)}, u32[]{:S(2)}) %all-to-all-start.2) | async-done | bytes 720928 | tf_op jit(solution)/shard_map/all_to_all | solution.py:230
  153.7 1.5 tile.25
  155.6 1.5 reshape.488
  157.6 1.5 reshape.492
  159.2 1.5 tile.22
  160.6 2.6 %multiply_add_fusion = (f32[3,32,1024]{2,1,0:T(8,128)S(1)}, f32[3,32,1024]{2,1,0:T(8,128)S(1)}) fusion(f32[3,32,1024]{2,1,0:T(8,128)S(1)} %add.421, f32[3,32,1023]{2,1,0:T(8,128)} %get-tuple-element.29, f32[3,32,1023]{2,1,0:T(8,128)} %get-tuple-element.28, f32[3,32,992]{2,1,0:T(8,128)} %get-tuple-element.27, f32[3,32,992]{2,1,0:T(8,128)S(1)} %get-tuple-element.26, ...), kind=kLoop, calls=%fused_computation.29 | loop fusion | flops 2359296 | bytes 5485888 | tf_op jit(solution)/shard_map/add | solution.py:49
  (195 shorter events, 30.7 us)
Async XLA Ops:
  3.2 23.7 %copy-start.11 = (pred[3,16]{1,0:T(4,128)(4,1)}, pred[3,16]{1,0:T(4,128)(4,1)S(1)}, u32[]{:S(2)}) copy-start(pred[3,16]{1,0:T(4,128)(4,1)S(1)} %fusion.56) | copy-start | bytes 148
  3.4 23.5 %copy-start.13 = (pred[3,2]{0,1:T(4,128)(4,1)}, pred[3,2]{0,1:T(4,128)(4,1)S(1)}, u32[]{:S(2)}) copy-start(pred[3,2]{0,1:T(4,128)(4,1)S(1)} %iota_compare_fusion.3) | copy-start | bytes 22
  4.2 24.8 %all-to-all-start = ((s32[16,2,2]{1,2,0:T(2,128)}), s32[16,2,2]{1,2,0:T(2,128)S(1)}, u32[]{:S(2)}, u32[]{:S(2)}) async-start(s32[16,2,2]{1,2,0:T(2,128)} %copy.106), calls=%async_computation | async-start | bytes 32768 | tf_op jit(solution)/shard_map/all_to_all | solution.py:150
  21.7 4.4 %copy-start.23 = (s32[256]{0:T(256)}, s32[256]{0:T(256)S(1)}, u32[]{:S(2)}) copy-start(s32[256]{0:T(256)S(1)} %get-tuple-element.50) | copy-start | bytes 3076
  21.7 4.4 %copy-start.25 = (s32[256]{0:T(256)}, s32[256]{0:T(256)S(1)}, u32[]{:S(2)}) copy-start(s32[256]{0:T(256)S(1)} %get-tuple-element.51) | copy-start | bytes 3076
  21.7 3.3 %copy-start.7 = (pred[1024]{0:T(1024)(128)(4,1)}, pred[1024]{0:T(1024)(128)(4,1)S(1)}, u32[]{:S(2)}) copy-start(pred[1024]{0:T(1024)(128)(4,1)S(1)} %get-tuple-element.47) | copy-start | bytes 3076
  21.7 3.3 %copy-start.9 = (pred[1024]{0:T(1024)(128)(4,1)}, pred[1024]{0:T(1024)(128)(4,1)S(1)}, u32[]{:S(2)}) copy-start(pred[1024]{0:T(1024)(128)(4,1)S(1)} %get-tuple-element.46) | copy-start | bytes 3076
  21.7 4.4 %copy-start.15 = (s32[1024]{0:T(1024)}, s32[1024]{0:T(1024)S(1)}, u32[]{:S(2)}) copy-start(s32[1024]{0:T(1024)S(1)} %get-tuple-element.48) | copy-start | bytes 12292
  21.7 4.4 %copy-start.17 = (s32[1024]{0:T(1024)}, s32[1024]{0:T(1024)S(1)}, u32[]{:S(2)}) copy-start(s32[1024]{0:T(1024)S(1)} %get-tuple-element.49) | copy-start | bytes 12292
  26.8 9.1 %copy-start.3 = (f32[32,32,128]{2,1,0:T(8,128)S(1)}, f32[32,32,128]{2,1,0:T(8,128)}, u32[]{:S(2)}) copy-start(f32[32,32,128]{2,1,0:T(8,128)} %param.5) | copy-start | bytes 1572868
  29.0 24.1 %all-to-all-start.1 = ((f32[16,2,4096]{2,1,0:T(2,128)}), f32[16,2,4096]{2,1,0:T(2,128)S(1)}, u32[]{:S(2)}, u32[]{:S(2)}) async-start(f32[16,2,4096]{2,1,0:T(2,128)} %copy.108), calls=%async_computation.1 | async-start | bytes 1048576 | tf_op jit(solution)/shard_map/all_to_all | solution.py:149
  48.3 8.5 %copy-start.19 = (s32[32]{0:T(128)}, s32[32]{0:T(128)S(1)}, u32[]{:S(2)}) copy-start(s32[32]{0:T(128)S(1)} %slice_bitcast_fusion) | copy-start | bytes 388
  48.3 8.5 %copy-start.21 = (pred[32]{0:T(512)(128)(4,1)}, pred[32]{0:T(512)(128)(4,1)S(1)}, u32[]{:S(2)}) copy-start(pred[32]{0:T(512)(128)(4,1)S(1)} %compare_bitcast_fusion) | copy-start | bytes 100
  66.7 2.6 %collective-permute-start = (f32[3,32,128]{2,1,0:T(8,128)S(1)}, f32[3,32,128]{2,1,0:T(8,128)S(1)}, u32[]{:S(2)}, u32[]{:S(2)}) collective-permute-start(f32[3,32,128]{2,1,0:T(8,128)S(1)} %get-tuple-element.17), channel_id=1, source_target_pairs={{0,128},{128,256},{256,384},{384,512},{512,640},{640,768},{768,896... | collective-permute-start | bytes 147464 | tf_op jit(solution)/shard_map/ppermute | solution.py:22
  68.0 4.8 %collective-permute-start.1 = (f32[3,32,128]{2,1,0:T(8,128)S(1)}, f32[3,32,128]{2,1,0:T(8,128)S(1)}, u32[]{:S(2)}, u32[]{:S(2)}) collective-permute-start(f32[3,32,128]{2,1,0:T(8,128)S(1)} %get-tuple-element.16), channel_id=1, source_target_pairs={{128,0},{256,128},{384,256},{512,384},{640,512},{768,640},{896,768... | collective-permute-start | bytes 147464 | tf_op jit(solution)/shard_map/ppermute | solution.py:24
  72.9 3.3 %collective-permute-start.2 = (f32[38,3,128]{2,1,0:T(4,128)S(1)}, f32[38,3,128]{2,1,0:T(4,128)S(1)}, u32[]{:S(2)}, u32[]{:S(2)}) collective-permute-start(f32[38,3,128]{2,1,0:T(4,128)S(1)} %get-tuple-element.14), channel_id=1, source_target_pairs={{0,16},{16,32},{32,48},{48,64},{64,80},{80,96},{96,112},{1,17},{17... | collective-permute-start | bytes 175112 | tf_op jit(solution)/shard_map/ppermute | solution.py:22
  74.2 5.8 %collective-permute-start.3 = (f32[38,3,128]{2,1,0:T(4,128)S(1)}, f32[38,3,128]{2,1,0:T(4,128)S(1)}, u32[]{:S(2)}, u32[]{:S(2)}) collective-permute-start(f32[38,3,128]{2,1,0:T(4,128)S(1)} %get-tuple-element.15), channel_id=1, source_target_pairs={{16,0},{32,16},{48,32},{64,48},{80,64},{96,80},{112,96},{17,1},{33... | collective-permute-start | bytes 175112 | tf_op jit(solution)/shard_map/ppermute | solution.py:24
  81.1 7.3 %collective-permute-start.5 = (f32[38,38,3]{1,0,2:T(8,128)S(1)}, f32[38,38,3]{1,0,2:T(8,128)S(1)}, u32[]{:S(2)}, u32[]{:S(2)}) collective-permute-start(f32[38,38,3]{1,0,2:T(8,128)S(1)} %copy.112), channel_id=1, source_target_pairs={{1,0},{2,1},{3,2},{4,3},{5,4},{6,5},{7,6},{8,7},{9,8},{10,9},{11,1... | collective-permute-start | bytes 51992 | tf_op jit(solution)/shard_map/ppermute | solution.py:24
  83.9 4.1 %collective-permute-start.4 = (f32[38,38,3]{1,0,2:T(8,128)S(1)}, f32[38,38,3]{1,0,2:T(8,128)S(1)}, u32[]{:S(2)}, u32[]{:S(2)}) collective-permute-start(f32[38,38,3]{1,0,2:T(8,128)S(1)} %copy.111), channel_id=1, source_target_pairs={{0,1},{1,2},{2,3},{3,4},{4,5},{5,6},{6,7},{7,8},{8,9},{9,10},{10,1... | collective-permute-start | bytes 51992 | tf_op jit(solution)/shard_map/ppermute | solution.py:22
  94.8 10.0 %copy-start.1 = (f32[32,32,128]{2,1,0:T(8,128)}, f32[32,32,128]{2,1,0:T(8,128)S(1)}, u32[]{:S(2)}) copy-start(f32[32,32,128]{2,1,0:T(8,128)S(1)} %slice.268) | copy-start | bytes 1572868
  101.9 2.1 %copy-start.2 = (f32[32,32,8]{2,1,0:T(8,128)S(1)}, f32[32,32,8]{2,1,0:T(8,128)}, u32[]{:S(2)}) copy-start(f32[32,32,8]{2,1,0:T(8,128)} %slice.230) | copy-start | bytes 98308
  112.3 4.8 %copy-start.5 = (f32[32,256]{1,0:T(8,128)S(1)}, f32[32,256]{1,0:T(8,128)}, u32[]{:S(2)}) copy-start(f32[32,256]{1,0:T(8,128)} %reshape.468) | copy-start | bytes 98308
  112.3 4.8 %copy-start.4 = (f32[32,256]{1,0:T(8,128)S(1)}, f32[32,256]{1,0:T(8,128)}, u32[]{:S(2)}) copy-start(f32[32,256]{1,0:T(8,128)} %reshape.474) | copy-start | bytes 98308
  112.3 4.9 %copy-start.20 = (s32[32]{0:T(128)S(1)}, s32[32]{0:T(128)}, u32[]{:S(2)}) copy-start(s32[32]{0:T(128)} %copy-done.19) | copy-start | bytes 388
  112.3 4.9 %copy-start.22 = (pred[32]{0:T(512)(128)(4,1)S(1)}, pred[32]{0:T(512)(128)(4,1)}, u32[]{:S(2)}) copy-start(pred[32]{0:T(512)(128)(4,1)} %copy-done.21) | copy-start | bytes 100
  117.7 29.1 %copy-start.12 = (pred[3,16]{1,0:T(4,128)(4,1)S(1)}, pred[3,16]{1,0:T(4,128)(4,1)}, u32[]{:S(2)}) copy-start(pred[3,16]{1,0:T(4,128)(4,1)} %copy-done.11) | copy-start | bytes 148
  117.7 29.1 %copy-start.14 = (pred[3,2]{0,1:T(4,128)(4,1)S(1)}, pred[3,2]{0,1:T(4,128)(4,1)}, u32[]{:S(2)}) copy-start(pred[3,2]{0,1:T(4,128)(4,1)} %copy-done.13) | copy-start | bytes 22
  117.7 29.6 %copy-start.16 = (s32[1024]{0:T(1024)S(1)}, s32[1024]{0:T(1024)}, u32[]{:S(2)}) copy-start(s32[1024]{0:T(1024)} %copy-done.15) | copy-start | bytes 12292
  117.8 29.6 %copy-start.18 = (s32[1024]{0:T(1024)S(1)}, s32[1024]{0:T(1024)}, u32[]{:S(2)}) copy-start(s32[1024]{0:T(1024)} %copy-done.17) | copy-start | bytes 12292
  117.8 29.6 %copy-start.24 = (s32[256]{0:T(256)S(1)}, s32[256]{0:T(256)}, u32[]{:S(2)}) copy-start(s32[256]{0:T(256)} %copy-done.23) | copy-start | bytes 3076
  117.8 29.6 %copy-start.26 = (s32[256]{0:T(256)S(1)}, s32[256]{0:T(256)}, u32[]{:S(2)}) copy-start(s32[256]{0:T(256)} %copy-done.25) | copy-start | bytes 3076
  119.1 27.8 %all-to-all-start.2 = ((f32[16,2,5632]{2,1,0:T(2,128)}), f32[16,2,5632]{2,1,0:T(2,128)S(1)}, u32[]{:S(2)}, u32[]{:S(2)}) async-start(f32[16,2,5632]{2,1,0:T(2,128)} %reshape.479), calls=%async_computation.2 | async-start | bytes 1441792 | tf_op jit(solution)/shard_map/all_to_all | solution.py:230
  (4 other events, 5.7 us)
where the time goes:
time: 167 us; the launch traced here: 165 us
  local copies, waits for them, and re-layouts  66.6 us (40%)
  starting transfers between devices  41.7 us (25%)
  waiting for transfers between devices  35.3 us (21%)
  other arithmetic  14.4 us (9%)
  matrix products  4.39 us (3%)
  between operations  2.29 us (1%)
    all_to_all x1, waiting for transfers between devices, per_device(): lax.all_to_all(outgoing_loop.reshape(group_size, CAP, -1), 'gz', split_ax...  21.3 us
    all_to_all x1, starting transfers between devices, per_device(): lax.all_to_all(labels, 'gz', split_axis=0, concat_axis=0, tiled=True)  17.4 us
    reshape x3, local copies, waits for them, and re-layouts, split_positions(): block_values.reshape(cells_first // foot_edge, foot_edge, cells_second //...  10.1 us
    reshape x2, local copies, waits for them, and re-layouts, merge_positions(): position_rows.reshape(cells_first // foot_edge, cells_second // foot_edge...  9.44 us
    reshape x2, local copies, waits for them, and re-layouts, split_positions(): return shaped.transpose(0, 2, 4, 1, 3, 5).reshape(-1, foot_edge ** 3)  9.42 us
    ppermute x3, waiting for transfers between devices, padded_2(): lax.ppermute(head, axis, [((i + 1) % count, i) for i in range(ends)])  7.3 us
    all_to_all x1, starting transfers between devices, per_device(): lax.all_to_all(outgoing, 'gz', split_axis=0, concat_axis=0, tiled=True)  6.89 us
    all_to_all x1, starting transfers between devices, per_device(): lax.all_to_all(outgoing_loop.reshape(group_size, CAP, -1), 'gz', split_ax...  6.43 us
  transfers between devices with their start and end apart: 9, of which 7 were waited for; matrix products, arithmetic and copies ran while one was open for 11% of the time, Pallas kernels for 0%

commit v1 on v0

v1 whole, which is shorter than its diff:
```python
import functools

import jax
import jax.numpy as jnp
from jax import lax
from jax.experimental import pallas as pl
from jax.experimental.pallas import tpu as pltpu
from jax.sharding import PartitionSpec as P

MESH = pl.DeviceIdType.MESH
SLOTS = 3
EDGE = 32
FOOT = 16
LANES = 128
SPOTS = 32
REC = 24


def iota(shape, dim):
    return lax.broadcasted_iota(jnp.int32, shape, dim)


def rolled(values, shift, axis):
    shift = shift % values.shape[axis]
    return values if shift == 0 else pltpu.roll(values, shift, axis)


def fine_sum(v):
    row = iota(v.shape, 0) % EDGE
    lane = iota(v.shape, 1)
    z = lane % EDGE
    total = jnp.where(row > 0, rolled(v, 1, 0), 0.0) + jnp.where(row < EDGE - 1, rolled(v, -1, 0), 0.0)
    total += jnp.where(lane >= EDGE, rolled(v, EDGE, 1), 0.0)
    total += jnp.where(lane < EDGE * (EDGE - 1), rolled(v, -EDGE, 1), 0.0)
    total += jnp.where(z > 0, rolled(v, 1, 1), 0.0)
    return total + jnp.where(z < EDGE - 1, rolled(v, -1, 1), 0.0)


def split3(v):
    high = v.astype(jnp.bfloat16)
    rest = v - high.astype(jnp.float32)
    middle = rest.astype(jnp.bfloat16)
    low = (rest - middle.astype(jnp.float32)).astype(jnp.bfloat16)
    return high, middle, low


def select_dot(v, chosen, dims):
    total = None
    for part in reversed(split3(v)):
        term = lax.dot_general(part, chosen, (dims, ((), ())), preferred_element_type=jnp.float32)
        total = term if total is None else total + term
    return total


def expand_matrix():
    lane = iota((1, EDGE * EDGE), 1)
    key = (lane // (2 * EDGE)) * FOOT + (lane % EDGE) // 2
    row = iota((FOOT * FOOT, EDGE * EDGE), 0)
    return jnp.where(row == key, 1.0, 0.0).astype(jnp.bfloat16)


def face_matrix():
    lane = iota((1, EDGE * EDGE), 1)
    y, z = lane // EDGE, lane % EDGE
    row = iota((LANES, EDGE * EDGE), 0) % 64
    hit = row == jnp.where(y == 0, z // 2, -1)
    hit |= row == jnp.where(y == EDGE - 1, FOOT + z // 2, -1)
    hit |= row == jnp.where(z == 0, 2 * FOOT + y // 2, -1)
    hit |= row == jnp.where(z == EDGE - 1, 3 * FOOT + y // 2, -1)
    return jnp.where(hit, 1.0, 0.0).astype(jnp.bfloat16)


def pre_kernel(count_ref, corner_ref, fine_ref, averages_ref, codes_ref, sums):
    row = iota((8, LANES), 0)
    codes = jnp.full((8, LANES), -1, jnp.int32)
    for slot in range(SLOTS):
        first, second, third = (corner_ref[slot, dim] for dim in range(3))
        spot = lax.div(lax.rem(first, EDGE), FOOT) * 2 + lax.div(lax.rem(second, EDGE), FOOT)
        spot = spot * 8 + lax.div(lax.rem(third, LANES), FOOT)
        code = jnp.where(slot < count_ref[0], lax.div(third, LANES) * SPOTS + spot, -1)
        codes = jnp.where(row == slot, code, codes)
    codes_ref[...] = codes
    right = fine_ref[...]
    pre = 0.165 * right + 0.0225 * fine_sum(right)
    residual = right - 6.0 * pre + fine_sum(pre)
    coarse = select_dot(residual, expand_matrix(), ((1,), (1,)))
    rows = SLOTS * FOOT
    for part in range(2):
        lanes = slice(part * LANES, (part + 1) * LANES)
        sums[part] = coarse[:, lanes]
        averages_ref[:, lanes] = 0.5 * (
            sums[part, pl.ds(0, rows, stride=2), :] + sums[part, pl.ds(1, rows, stride=2), :]
        )


def post_kernel(count_ref, fine_ref, record_ref, out_ref, parent, faces):
    right = fine_ref[...]
    pre = 0.165 * right + 0.0225 * fine_sum(right)
    lane = iota((FOOT, LANES), 1)
    low_rows, high_rows = [], []
    for slot in range(SLOTS):
        first = slot * REC
        for odd in range(2):
            for part in range(2):
                parent[part, pl.ds(slot * EDGE + odd, FOOT, stride=2), :] = record_ref[
                    pl.ds(first, FOOT), part * LANES : (part + 1) * LANES
                ]
        tile = record_ref[pl.ds(first + FOOT, 8), 0:LANES]
        for odd in range(2):
            faces[pl.ds(slot * EDGE + odd, 8, stride=2), :] = tile
            faces[pl.ds(slot * EDGE + FOOT + odd, 8, stride=2), :] = tile
        side = record_ref[pl.ds(first + FOOT, 8), LANES : 2 * LANES]
        low_rows.append(jnp.concatenate([side[0:1], side[1:2]], 1))
        high_rows.append(jnp.concatenate([side[2:3], side[3:4]], 1))
    expand = expand_matrix()
    lifted = select_dot(jnp.concatenate([parent[0], parent[1]], 1), expand, ((1,), (0,)))
    row = iota((SLOTS * EDGE, LANES), 0) % EDGE
    wanted = (row >= FOOT) == (iota((SLOTS * EDGE, LANES), 1) >= 64)
    ghost = select_dot(jnp.where(wanted, faces[...], 0.0), face_matrix(), ((1,), (0,)))
    spare = jnp.zeros((2, FOOT * FOOT), jnp.float32)
    ends = select_dot(jnp.concatenate(low_rows + high_rows + [spare], 0), expand, ((1,), (0,)))
    value = pre + lifted
    row = iota((EDGE, EDGE * EDGE), 0)
    count = count_ref[0]
    for slot in range(SLOTS):
        rows = slice(slot * EDGE, (slot + 1) * EDGE)
        now = value[rows]
        fixed = right[rows] + ghost[rows]
        fixed += jnp.where(row == 0, ends[slot : slot + 1], 0.0)
        fixed += jnp.where(row == EDGE - 1, ends[SLOTS + slot : SLOTS + slot + 1], 0.0)
        for _ in range(2):
            now = 0.1 * now + 0.15 * (fixed + fine_sum(now))
        out_ref[rows, :] = jnp.where(slot < count, now, 0.0)


def coarse_kernel(
    sizes,
    codes_ref,
    averages_ref,
    coarse_ref,
    solution_ref,
    record_ref,
    gathered,
    meta,
    table,
    table_smem,
    level1,
    level2,
    level3,
    x_out,
    x_in,
    z_out,
    z_in,
    records,
    pre_out,
    pre_in,
    chain_out,
    chain_in,
    ring_send,
    ring_recv,
    pair_send,
    pair_recv,
    halo_send,
    halo_recv,
    pre_send,
    pre_recv,
    chain_send,
    chain_recv,
    table_sem,
):
    n_x, n_y, n_z = sizes
    chips = n_z // 2
    half = chips // 2
    gx, gy, me = lax.axis_index("gx"), lax.axis_index("gy"), lax.axis_index("gz")
    chip, core = lax.div(me, 2), lax.rem(me, 2)
    sign = 1 - 2 * core
    pair = me + sign
    ring = tuple(lax.rem(chip + step * sign + chips, chips) * 2 + core for step in (1, -1))
    z_near = tuple(lax.rem(me + step + n_z, n_z) for step in (-1, 1))
    y_near = tuple(lax.rem(gy + step + n_y, n_y) for step in (-1, 1))
    x_near = tuple(lax.rem(gx + step + n_x, n_x) for step in (-1, 1))
    lane = iota((FOOT, LANES), 1)
    group = lane // FOOT

    barrier = pltpu.get_barrier_semaphore()
    greeted = [{"gz": d} for d in ring + z_near] + [{"gy": d} for d in y_near] + [{"gx": d} for d in x_near]
    for device in greeted:
        pl.semaphore_signal(barrier, inc=1, device_id=device, device_id_type=MESH)

    row8 = iota((8, LANES), 0)
    meta[me] = codes_ref[...]
    for slot in range(SLOTS):
        gathered[me * SLOTS + slot] = averages_ref[pl.ds(slot * FOOT, FOOT), :]
    pl.semaphore_wait(barrier, len(greeted))

    def send(source, target, send_sem, recv_sem, device):
        copy = pltpu.make_async_remote_copy(
            src_ref=source,
            dst_ref=target,
            send_sem=send_sem,
            recv_sem=recv_sem,
            device_id=device,
            device_id_type=MESH,
        )
        copy.start()
        return copy

    started = []

    items = (SLOTS,) + tuple(range(SLOTS))
    takes = ((SLOTS, 0, 1), (2,))

    def carried(way, hop, item):
        return hop < half or item in takes[way]

    def place(owner, item):
        return meta.at[owner] if item == SLOTS else gathered.at[owner * SLOTS + item]

    def owner_of(way, hop):
        step = hop if way == 0 else -hop
        return lax.rem(chip - step * sign + chips, chips) * 2 + core

    ring_copies, pair_copies = {}, []
    for item in items:
        for way in range(2):
            if carried(way, 1, item):
                ring_copies[way, 1, item] = send(
                    place(me, item),
                    place(me, item),
                    ring_send.at[way, 0, item],
                    ring_recv.at[way, 0, item],
                    {"gz": ring[way]},
                )
        pair_copies.append(
            send(place(me, item), place(me, item), pair_send.at[0, 0, item], pair_recv.at[0, 0, item], {"gz": pair})
        )
    for hop in range(1, half + 1):
        for item in items:
            for way in range(2):
                if not carried(way, hop, item):
                    continue
                ring_copies[way, hop, item].wait_recv()
                here = place(owner_of(way, hop), item)
                if hop < half and carried(way, hop + 1, item):
                    ring_copies[way, hop + 1, item] = send(
                        here,
                        here,
                        ring_send.at[way, hop, item],
                        ring_recv.at[way, hop, item],
                        {"gz": ring[way]},
                    )
                pair_copies.append(
                    send(here, here, pair_send.at[way, hop, item], pair_recv.at[way, hop, item], {"gz": pair})
                )
    started += list(ring_copies.values()) + pair_copies
    for number, copy in enumerate(pair_copies):
        copy.wait_recv()

    lane8 = iota((8, LANES), 1)
    sources = jnp.zeros((8, LANES), jnp.int32)
    spots = jnp.full((8, LANES), SPOTS, jnp.int32)
    for owner in range(n_z):
        codes = meta[owner] - me * SPOTS
        live = (codes >= 0) & (codes < SPOTS) & (row8 < SLOTS)
        hit = live & (codes == lane8)
        sources = jnp.maximum(sources, jnp.where(hit, owner * SLOTS + row8 + 1, 0))
        spots = jnp.where((lane8 == owner) & live, codes, spots)
    source = jnp.maximum(jnp.maximum(sources[0:1], sources[1:2]), sources[2:3])
    source = jnp.broadcast_to(source, (8, LANES))
    covers = jnp.where(source > 0, lane8 % 8, -1)
    table[pl.ds(0, 8), :] = jnp.where(row8 == 0, jnp.maximum(source - 1, 0), covers)
    table[pl.ds(8, 8), :] = spots
    table_copy = pltpu.make_async_copy(table, table_smem, table_sem)
    table_copy.start()
    table_copy.wait()

    for sx in range(2):
        for sy in range(2):
            cubes, masks = [], []
            for sz in range(8):
                spot = (sx * 2 + sy) * 8 + sz
                cubes.append(gathered[table_smem[0, spot]])
                masks.append(group == table_smem[1, spot])
            for second in range(FOOT):
                part, place_in = second // 8, second % 8
                y = sy * FOOT + second
                plane = coarse_ref[pl.ds(sx * FOOT * EDGE + y, FOOT, stride=EDGE), :]
                for sz in range(8):
                    cube = cubes[sz][:, part * LANES : (part + 1) * LANES]
                    plane = jnp.where(masks[sz], rolled(cube, FOOT * (sz - place_in), 1), plane)
                level1[pl.ds((y + 1) * EDGE + sx * FOOT, FOOT), :] = plane

    lane32 = iota((EDGE, LANES), 1)
    row32 = iota((EDGE, LANES), 0)

    def start_halo(number, level):
        x_out[number, 0] = level[pl.ds(EDGE, EDGE, stride=EDGE), :]
        x_out[number, 1] = level[pl.ds(EDGE + EDGE - 1, EDGE, stride=EDGE), :]
        low = jnp.zeros((EDGE, LANES), jnp.float32)
        high = jnp.zeros((EDGE, LANES), jnp.float32)
        for y in range(EDGE):
            plane = level[pl.ds((y + 1) * EDGE, EDGE), :]
            low = jnp.where(lane32 == y, rolled(plane, y, 1), low)
            high = jnp.where(lane32 == y, rolled(plane, y - (LANES - 1), 1), high)
        z_out[number, 0] = low
        z_out[number, 1] = high
        copies = []
        for side in range(2):
            other = 1 - side
            copies.append(
                send(
                    x_out.at[number, side],
                    x_in.at[number, other],
                    halo_send.at[number, side],
                    halo_recv.at[number, other],
                    {"gx": x_near[side]},
                )
            )
            copies.append(
                send(
                    level.at[pl.ds(EDGE if side == 0 else EDGE * EDGE, EDGE)],
                    level.at[pl.ds((EDGE + 1) * EDGE if side == 0 else 0, EDGE)],
                    halo_send.at[number, 2 + side],
                    halo_recv.at[number, 2 + other],
                    {"gy": y_near[side]},
                )
            )
            copies.append(
                send(
                    z_out.at[number, side],
                    z_in.at[number, other],
                    halo_send.at[number, 4 + side],
                    halo_recv.at[number, 4 + other],
                    {"gz": z_near[side]},
                )
            )
        return copies

    def finish_halo(number, level, copies):
        for copy in copies:
            copy.wait_recv()
        started.extend(copies)
        for side in range(2):
            inside = (gx > 0, gy > 0, me > 0) if side == 0 else (gx < n_x - 1, gy < n_y - 1, me < n_z - 1)
            x_in[number, side] = jnp.where(inside[0], x_in[number, side], 0.0)
            edge = pl.ds(0 if side == 0 else (EDGE + 1) * EDGE, EDGE)
            level[edge, :] = jnp.where(inside[1], level[edge, :], 0.0)
            z_in[number, side] = jnp.where(inside[2], z_in[number, side], 0.0)

    def sweep(number, level, out, weights):
        z_low, z_high = z_in[number, 0], z_in[number, 1]
        for y in range(EDGE):
            plane = level[pl.ds((y + 1) * EDGE, EDGE), :]
            total = level[pl.ds(y * EDGE, EDGE), :] + level[pl.ds((y + 2) * EDGE, EDGE), :]
            x_low, x_high = x_in[number, 0, pl.ds(y, 1), :], x_in[number, 1, pl.ds(y, 1), :]
            total += jnp.where(row32 == 0, x_low, rolled(plane, 1, 0))
            total += jnp.where(row32 == EDGE - 1, x_high, rolled(plane, -1, 0))
            total += jnp.where(lane32 == 0, rolled(z_low, -y, 1), rolled(plane, 1, 1))
            total += jnp.where(
                lane32 == LANES - 1, rolled(z_high, LANES - 1 - y, 1), rolled(plane, -1, 1)
            )
            if weights is None:
                value = 0.165 * plane + 0.0225 * total
            else:
                value = 0.1 * plane + 0.15 * (level1[pl.ds((y + 1) * EDGE, EDGE), :] + total)
            out[pl.ds((y + 1) * EDGE, EDGE), :] = value
            if weights is not None:
                solution_ref[pl.ds(y, EDGE, stride=EDGE), :] = value

    copies = start_halo(0, level1)
    finish_halo(0, level1, copies)
    sweep(0, level1, level2, None)
    copies = start_halo(1, level2)
    finish_halo(1, level2, copies)
    sweep(1, level2, level3, 1)
    copies = start_halo(2, level3)
    finish_halo(2, level3, copies)

    for sx in range(2):
        rows = pl.ds(sx * FOOT, FOOT)
        for sy in range(2):
            planes = [
                level3[pl.ds((sy * FOOT + second) * EDGE + sx * FOOT, FOOT), :] for second in range(FOOT + 2)
            ]
            upper = jnp.zeros((FOOT, LANES), jnp.float32)
            lower = jnp.zeros((FOOT, LANES), jnp.float32)
            for second in range(FOOT):
                here = lane % FOOT == second
                upper = jnp.where(here, rolled(planes[second + 1], second - (FOOT - 1), 1), upper)
                lower = jnp.where(here, rolled(planes[second + 1], second, 1), lower)
            ends = []
            for side in range(2):
                if side == sx:
                    face = x_in[2, side, pl.ds(sy * FOOT, FOOT), :]
                else:
                    x = FOOT - 1 if side == 0 else FOOT
                    face = level3[pl.ds((sy * FOOT + 1) * EDGE + x, FOOT, stride=EDGE), :]
                for part in range(2):
                    tile = face[part * 8 : part * 8 + 8]
                    turned = jnp.zeros((8, LANES), jnp.float32)
                    for step in range(8):
                        moved = rolled(rolled(tile, -step, 0), FOOT * step, 1)
                        turned = jnp.where((lane8 // FOOT - row8 + 8) % 8 == step, moved, turned)
                    ends.append(turned)
            for sz in range(8):
                spot = (sx * 2 + sy) * 8 + sz
                for part in range(2):
                    cube = jnp.zeros((FOOT, LANES), jnp.float32)
                    for second in range(8):
                        moved = rolled(planes[part * 8 + second + 1], FOOT * (second - sz), 1)
                        cube = jnp.where(group == second, moved, cube)
                    records[spot, pl.ds(0, FOOT), part * LANES : (part + 1) * LANES] = cube
                if sz > 0:
                    z_low = rolled(upper, 2 * FOOT - FOOT * (sz - 1), 1)
                else:
                    z_low = rolled(z_in[2, 0, rows, :], 2 * FOOT - FOOT * sy, 1)
                if sz < 7:
                    z_high = rolled(lower, 3 * FOOT - FOOT * (sz + 1), 1)
                else:
                    z_high = rolled(z_in[2, 1, rows, :], 3 * FOOT - FOOT * sy, 1)
                face = jnp.where(group == 0, rolled(planes[0], -FOOT * sz, 1), 0.0)
                face = jnp.where(group == 1, rolled(planes[FOOT + 1], FOOT - FOOT * sz, 1), face)
                face = jnp.where(group == 2, z_low, face)
                face = jnp.where(group == 3, z_high, face)
                records[spot, pl.ds(FOOT, 8), 0:LANES] = face[0:8] + rolled(face[8:16], 64, 1)
                side_rows = jnp.zeros((8, LANES), jnp.float32)
                for number, turned in enumerate(ends):
                    side_rows = jnp.where(row8 == number, turned[sz : sz + 1], side_rows)
                records[spot, pl.ds(FOOT, 8), LANES : 2 * LANES] = side_rows

    records[SPOTS] = jnp.zeros((REC, FOOT * FOOT), jnp.float32)

    def own(owner, slot):
        return records[table_smem[8 + slot, owner]]

    def chip_at(step):
        return lax.rem(chip + step + chips, chips)

    places = [(0, half)]
    for left in range(half - 1, 0, -1):
        places += [(0, left), (1, left)]
    places.append((0, 0))
    number_of = {key: number for number, key in enumerate(places)}
    number_of[1, half] = number_of[0, half]
    number_of[1, 0] = number_of[0, 0]

    def step_of(way, left):
        return left if way == 0 else -left

    pre_copies = []
    for number, (way, left) in enumerate(places):
        target = chip_at(-sign * step_of(way, left)) * 2 + 1 - core
        for slot in range(SLOTS):
            pre_out[number, pl.ds(slot * REC, REC), :] = own(target, slot)
        pre_copies.append(
            send(pre_out.at[number], pre_in.at[number], pre_send.at[number], pre_recv.at[number], {"gz": pair})
        )
    started += pre_copies

    def begins(way, slot):
        return half if slot in takes[way] else half - 1

    arrived = set()
    chain_copies = {}
    for left in range(half, 0, -1):
        for way in range(2):
            number = number_of[way, left]
            target = chip_at(sign * step_of(way, left)) * 2 + core
            for slot in range(SLOTS):
                if left > begins(way, slot):
                    continue
                if number not in arrived:
                    pre_copies[number].wait_recv()
                    arrived.add(number)
                value = own(target, slot) + pre_in[number, pl.ds(slot * REC, REC), :]
                if left < begins(way, slot):
                    chain_copies[way, left, slot].wait_recv()
                    value += chain_in[way, left, slot]
                chain_out[way, left - 1, slot] = value
                chain_copies[way, left - 1, slot] = send(
                    chain_out.at[way, left - 1, slot],
                    chain_in.at[way, left - 1, slot],
                    chain_send.at[way, left - 1, slot],
                    chain_recv.at[way, left - 1, slot],
                    {"gz": ring[way]},
                )
    started += list(chain_copies.values())
    number = number_of[0, 0]
    pre_copies[number].wait_recv()
    for slot in range(SLOTS):
        value = own(me, slot) + pre_in[number, pl.ds(slot * REC, REC), :]
        for way in range(2):
            if begins(way, slot) > 0:
                chain_copies[way, 0, slot].wait_recv()
                value += chain_in[way, 0, slot]
        record_ref[pl.ds(slot * REC, REC), :] = value
    for copy in started:
        copy.wait_send()


def vmem():
    return pl.BlockSpec(memory_space=pltpu.VMEM)


def smem():
    return pl.BlockSpec(memory_space=pltpu.SMEM)


def per_device(sizes, fine_rhs, coarse_rhs, patch_count, patch_corner):
    n_z = sizes[2]
    half = n_z // 4
    f32 = jnp.float32
    fine = fine_rhs.reshape(SLOTS * EDGE, EDGE * EDGE)
    averages, codes = pl.pallas_call(
        pre_kernel,
        out_shape=(
            jax.ShapeDtypeStruct((SLOTS * FOOT, FOOT * FOOT), f32),
            jax.ShapeDtypeStruct((8, LANES), jnp.int32),
        ),
        in_specs=[smem(), smem(), vmem()],
        out_specs=(vmem(), vmem()),
        scratch_shapes=[pltpu.VMEM((2, SLOTS * EDGE, LANES), f32)],
        name="pre",
    )(patch_count, patch_corner, fine)
    rows = EDGE * EDGE
    padded = (EDGE + 2) * EDGE
    record = SLOTS * REC
    dma = pltpu.SemaphoreType.DMA
    coarse_solution, loops = pl.pallas_call(
        functools.partial(coarse_kernel, sizes),
        out_shape=(
            jax.ShapeDtypeStruct((rows, LANES), f32),
            jax.ShapeDtypeStruct((record, FOOT * FOOT), f32),
        ),
        in_specs=[vmem(), vmem(), vmem()],
        out_specs=(vmem(), vmem()),
        scratch_shapes=[
            pltpu.VMEM((n_z * SLOTS, FOOT, FOOT * FOOT), f32),
            pltpu.VMEM((n_z, 8, LANES), jnp.int32),
            pltpu.VMEM((16, LANES), jnp.int32),
            pltpu.SMEM((16, LANES), jnp.int32),
            pltpu.VMEM((padded, LANES), f32),
            pltpu.VMEM((padded, LANES), f32),
            pltpu.VMEM((padded, LANES), f32),
            pltpu.VMEM((3, 2, EDGE, LANES), f32),
            pltpu.VMEM((3, 2, EDGE, LANES), f32),
            pltpu.VMEM((3, 2, EDGE, LANES), f32),
            pltpu.VMEM((3, 2, EDGE, LANES), f32),
            pltpu.VMEM((SPOTS + 1, REC, FOOT * FOOT), f32),
            pltpu.VMEM((2 * half, record, FOOT * FOOT), f32),
            pltpu.VMEM((2 * half, record, FOOT * FOOT), f32),
            pltpu.VMEM((2, half, SLOTS, REC, FOOT * FOOT), f32),
            pltpu.VMEM((2, half, SLOTS, REC, FOOT * FOOT), f32),
            dma((2, half, SLOTS + 1)),
            dma((2, half, SLOTS + 1)),
            dma((2, half + 1, SLOTS + 1)),
            dma((2, half + 1, SLOTS + 1)),
            dma((3, 6)),
            dma((3, 6)),
            dma((2 * half,)),
            dma((2 * half,)),
            dma((2, half, SLOTS)),
            dma((2, half, SLOTS)),
            dma,
        ],
        compiler_params=pltpu.CompilerParams(
            collective_id=0, has_side_effects=True, vmem_limit_bytes=32 * 1024 * 1024
        ),
        name="coarse",
    )(codes, averages, coarse_rhs.reshape(rows, LANES))
    fine_solution = pl.pallas_call(
        post_kernel,
        out_shape=jax.ShapeDtypeStruct(fine.shape, f32),
        in_specs=[smem(), vmem(), vmem()],
        out_specs=vmem(),
        scratch_shapes=[
            pltpu.VMEM((2, SLOTS * EDGE, LANES), f32),
            pltpu.VMEM((SLOTS * EDGE, LANES), f32),
        ],
        name="post",
    )(patch_count, fine, loops)
    return fine_solution.reshape(fine_rhs.shape), coarse_solution.reshape(coarse_rhs.shape)


def solution(mesh):
    sizes = tuple(mesh.shape[axis] for axis in ("gx", "gy", "gz"))
    return jax.shard_map(
        functools.partial(per_device, sizes),
        mesh=mesh,
        in_specs=(
            P(("gx", "gy", "gz"), None, None),
            P("gx", "gy", "gz"),
            P(("gx", "gy", "gz")),
            P(("gx", "gy", "gz"), None),
        ),
        out_specs=(P(("gx", "gy", "gz"), None, None), P("gx", "gy", "gz")),
        check_vma=False,
    )
```

time: 167 us -> 81.7 us (0.49); the launches traced: 165 us -> 81.3 us
  Pallas kernels: 0 us -> 76.1 us
  local copies, waits for them, and re-layouts: 66.6 us -> 3.95 us
  starting transfers between devices: 41.7 us -> 0 us
  waiting for transfers between devices: 35.3 us -> 0 us
  other arithmetic: 14.4 us -> 0 us
  matrix products: 4.39 us -> 0 us
    pallas_call x0 -> x3, Pallas kernels: none -> 76.1 us  [the longest x1 69.3 us: per_device(): pl.pallas_call(functools.partial(coarse_kernel, sizes), out_shape=(jax.Sh...]
    reshape x38 -> x0, local copies, waits for them, and re-layouts: 41.2 us -> none  [the longest x3 10.1 us: split_positions(): block_values.reshape(cells_first // foot_edge, foot_edge, cells_second //...]
    all_to_all x3 -> x0, starting transfers between devices: 30.7 us -> none  [the longest x1 17.4 us: per_device(): lax.all_to_all(labels, 'gz', split_axis=0, concat_axis=0, tiled=True)]
    all_to_all x3 -> x0, waiting for transfers between devices: 26.4 us -> none  [the longest x1 21.3 us: per_device(): lax.all_to_all(outgoing_loop.reshape(group_size, CAP, -1), 'gz', split_ax...]
    slice x28 -> x0, local copies, waits for them, and re-layouts: 12 us -> none  [the longest x1 2.98 us: per_device(): padded[1:cells_first + 1, 1:cells_second + 1, foot_edge + 1:cells_third +...]
    ppermute x6 -> x0, starting transfers between devices: 11 us -> none  [the longest x3 5.62 us: padded_2(): lax.ppermute(tail, axis, [(i, (i + 1) % count) for i in range(ends)])]
    ppermute x6 -> x0, waiting for transfers between devices: 8.95 us -> none  [the longest x3 7.3 us: padded_2(): lax.ppermute(head, axis, [((i + 1) % count, i) for i in range(ends)])]
    mul x3 -> x0, other arithmetic: 6.04 us -> none  [the longest x2 4.9 us: per_device(): iterate = iterate * inside]
  transfers between devices with their start and end apart: 9 -> 0, of which waited for: 7 -> 0; matrix products, arithmetic and copies ran while one was open for 11% -> 0% of each run, Pallas kernels for 0% -> 0%
where the time goes in v1:
time: 81.7 us; the launch traced here: 81.3 us
  Pallas kernels  76.1 us (93%)
  local copies, waits for them, and re-layouts  3.95 us (5%)
  between operations  1.3 us (2%)
    pallas_call x1, Pallas kernels, per_device(): pl.pallas_call(functools.partial(coarse_kernel, sizes), out_shape=(jax.Sh...  69.3 us
    unnamed x9, local copies, waits for them, and re-layouts  3.95 us
    pallas_call x1, Pallas kernels, per_device(): pl.pallas_call(post_kernel, out_shape=jax.ShapeDtypeStruct(fine.shape, f3...  3.71 us
    pallas_call x1, Pallas kernels, per_device(): pl.pallas_call(pre_kernel, out_shape=(jax.ShapeDtypeStruct((SLOTS * FOOT,...  3.13 us

profile of v1, /device:TPU:1, one launch (start us, length us, event | category | flops | bytes accessed | tf_op | source)
XLA Modules:
  0.0 81.3 jit_solution(2901343137452862503)
XLA Ops:
  1.3 3.1 %pre.1 = (f32[48,256]{1,0:T(8,128)}, s32[8,128]{1,0:T(8,128)}) custom-call(s32[1]{0:T(128)S(6)} %copy.7.count_ref, s32[3,3]{1,0:T(4,128)} %corner_ref.1, f32[96,1024]{1,0:T(8,128)} %bitcast.6), custom_call_target="tpu_custom_call" | custom-call | tf_op jit(solution)/shard_map/pre/pallas_call | solution.py:514
  4.4 0.0 copy-start
  4.4 1.0 %copy-done = f32[32,32,128]{2,1,0:T(8,128)S(1)} copy-done((f32[32,32,128]{2,1,0:T(8,128)S(1)}, f32[32,32,128]{2,1,0:T(8,128)}, u32[]{:S(2)}) %copy-start) | copy-done | bytes 524312
  5.5 0.0 copy-start.2
  5.5 0.8 copy-done.2
  6.3 0.0 copy-start.3
  6.3 0.7 copy-done.3
  6.9 69.3 %coarse.1 = (f32[1024,128]{1,0:T(8,128)S(1)}, f32[72,256]{1,0:T(8,128)S(1)}) custom-call(s32[8,128]{1,0:T(8,128)S(1)} %copy-done.3, f32[48,256]{1,0:T(8,128)S(1)} %copy-done.2, f32[1024,128]{1,0:T(8,128)S(1)} %bitcast.4), custom_call_target="tpu_custom_call" | custom-call | tf_op jit(solution)/shard_map/coarse/pallas_call | solution.py:529
  76.2 0.0 copy-start.1
  76.2 0.6 copy-done.1
  76.8 3.7 %post.1 = f32[96,1024]{1,0:T(8,128)} custom-call(s32[1]{0:T(128)S(6)} %copy.7.count_ref, f32[96,1024]{1,0:T(8,128)} %bitcast.7, f32[72,256]{1,0:T(8,128)} %copy-done.1), custom_call_target="tpu_custom_call" | custom-call | tf_op jit(solution)/shard_map/post/pallas_call | solution.py:571
  80.5 0.8 copy.8
Async XLA Ops:
  4.4 1.0 %copy-start = (f32[32,32,128]{2,1,0:T(8,128)S(1)}, f32[32,32,128]{2,1,0:T(8,128)}, u32[]{:S(2)}) copy-start(f32[32,32,128]{2,1,0:T(8,128)} %param.5) | copy-start | bytes 1572868
  5.5 0.8 copy-start.2
  6.3 0.7 copy-start.3
  76.2 0.6 copy-start.1
